TPU v7x, 32 devices: a whole 2x2x4 slice. The times are simulated.
32 devices in a mesh: seq: 8 (over z, y), rep: 4 (over x, core).
Axes of the slice: x: 2, y: 2, z: 4, core: 2. Of those that a mesh axis runs over, the one named last changes fastest.
Arguments:
- query_rows: bfloat16 [12288, 1024], P(('seq', 'rep')), may hold values from -6 to 6
- key_rows: bfloat16 [12288, 128], P(('seq', 'rep')), may hold values from -6 to 6
- value_rows: bfloat16 [12288, 128], P(('seq', 'rep')), may hold values from -6 to 6
- out_grad: bfloat16 [12288, 1024], P(('seq', 'rep')), may hold values from -1.5 to 1.5
- logsumexp: float32 [8, 12288], P(None, ('seq', 'rep')), may hold values from 1 to 3
- row_delta: float32 [8, 12288], P(None, ('seq', 'rep')), may hold values from -8 to 8
- doc_lengths: int32 [31], replicated, may hold values from 1 to 1537, as said below
Outputs:
- query_grad: bfloat16 [12288, 1024], P(('seq', 'rep'))
- key_grad: bfloat16 [12288, 128], P(('seq', 'rep'))
- value_grad: bfloat16 [12288, 128], P(('seq', 'rep'))
Inputs may be any that keep to these rules, and one draw needn't show every extreme that they name: `doc_lengths`: 31 document lengths in pack order, summing to 12288; so every document lies within 5 consecutive aligned blocks of 384 positions.
All inputs are finite; a program needn't handle non-finite values.
Results may differ from a plain program's by a relative error of at most 0.019.
Values may be sent and summed in bfloat16 or wider, within the bound.
A program may use at most 64 MiB of HBM per device.

v0:
```python
import jax
import jax.numpy as jnp
from jax import lax
from jax.sharding import PartitionSpec as P

REACH = 4


def from_behind(array, axis, by):
    length = lax.axis_size(axis)
    pairs = [(i, i + by) for i in range(length) if 0 <= i + by < length]
    return lax.ppermute(array, axis, pairs)


def doc_index(positions, doc_ends):
    return jnp.sum((doc_ends[None, :] <= positions[:, None]).astype(jnp.int32), axis=1)


def block_grads(
    query_block,
    grad_block,
    stat_block,
    delta_block,
    key_block,
    value_block,
    query_docs,
    key_docs,
    query_pos,
    key_pos,
):
    row_count = query_block.shape[0]
    head_size = key_block.shape[1]
    head_count = query_block.shape[1] // head_size
    score_scale = head_size ** (-0.5)
    query_heads = query_block.reshape(row_count, head_count, head_size)
    grad_heads = grad_block.reshape(row_count, head_count, head_size)
    scores = (
        jnp.einsum("qhd,kd->hqk", query_heads, key_block, preferred_element_type=jnp.float32)
        * score_scale
    )
    allowed = (query_docs[:, None] == key_docs[None, :]) & (key_pos[None, :] <= query_pos[:, None])
    probs = jnp.where(allowed[None], jnp.exp(scores - stat_block[:, :, None]), 0.0)
    dprobs = jnp.einsum("qhd,kd->hqk", grad_heads, value_block, preferred_element_type=jnp.float32)
    dscores = probs * (dprobs - delta_block[:, :, None])
    dscores_half = dscores.astype(jnp.bfloat16)
    query_part = (
        jnp.einsum("hqk,kd->qhd", dscores_half, key_block, preferred_element_type=jnp.float32)
        * score_scale
    ).reshape(row_count, head_count * head_size)
    probs_half = probs.astype(jnp.bfloat16)
    key_part = (
        jnp.einsum("hqk,qhd->kd", dscores_half, query_heads, preferred_element_type=jnp.float32)
        * score_scale
    )
    value_part = jnp.einsum(
        "hqk,qhd->kd", probs_half, grad_heads, preferred_element_type=jnp.float32
    )
    return (query_part, key_part, value_part)


def shards(query_rows, key_rows, value_rows, out_grad, logsumexp, row_delta, doc_lengths):
    shard_rows = query_rows.shape[0]
    first_row = lax.axis_index(("seq", "rep")) * shard_rows
    doc_ends = jnp.cumsum(doc_lengths)
    own_pos = first_row + jnp.arange(shard_rows, dtype=jnp.int32)
    own_docs = doc_index(own_pos, doc_ends)
    query_total, key_total, value_total = block_grads(
        query_rows,
        out_grad,
        logsumexp,
        row_delta,
        key_rows,
        value_rows,
        own_docs,
        own_docs,
        own_pos,
        own_pos,
    )
    for distance in range(1, REACH + 1):
        prev_pos = own_pos - distance * shard_rows
        prev_docs = jnp.where(prev_pos >= 0, doc_index(prev_pos, doc_ends), -1)
        prev_key, prev_value = from_behind((key_rows, value_rows), ("seq", "rep"), distance)
        cross_q, cross_k, cross_v = block_grads(
            query_rows,
            out_grad,
            logsumexp,
            row_delta,
            prev_key,
            prev_value,
            own_docs,
            prev_docs,
            own_pos,
            prev_pos,
        )
        extra_k, extra_v = (
            from_behind(cross_k.astype(jnp.bfloat16), ("seq", "rep"), -distance).astype(
                cross_k.dtype
            ),
            from_behind(cross_v.astype(jnp.bfloat16), ("seq", "rep"), -distance).astype(
                cross_v.dtype
            ),
        )
        query_total = query_total + cross_q
        key_total = key_total + extra_k
        value_total = value_total + extra_v
    return (
        query_total.astype(jnp.bfloat16),
        key_total.astype(jnp.bfloat16),
        value_total.astype(jnp.bfloat16),
    )


def solution(mesh):
    return jax.shard_map(
        shards,
        mesh=mesh,
        in_specs=(
            P(("seq", "rep"), None),
            P(("seq", "rep"), None),
            P(("seq", "rep"), None),
            P(("seq", "rep"), None),
            P(None, ("seq", "rep")),
            P(None, ("seq", "rep")),
            P(),
        ),
        out_specs=(P(("seq", "rep"), None), P(("seq", "rep"), None), P(("seq", "rep"), None)),
        check_vma=False,
    )
```

profile of v0, /device:TPU:29, one launch (start us, length us, event | category | flops | bytes accessed | tf_op | source)
XLA Modules:
  0.0 89.3 jit_solution(17576152254105893925)
XLA Ops:
  0.7 3.3 %collective-permute-start.3 = (bf16[384,128]{1,0:T(8,128)(2,1)}, bf16[384,128]{1,0:T(8,128)(2,1)S(1)}, u32[]{:S(2)}, u32[]{:S(2)}) collective-permute-start(bf16[384,128]{1,0:T(8,128)(2,1)} %param.9), channel_id=1, source_target_pairs={{0,2},{1,3},{2,4},{3,5},{4,6},{5,7},{6,8},{7,9},{8,10},{9,11},{10,... | collective-permute-start | bytes 294920 | tf_op jit(solution)/shard_map/ppermute | solution.py:12
  3.9 1.9 %collective-permute-start.1 = (bf16[384,128]{1,0:T(8,128)(2,1)}, bf16[384,128]{1,0:T(8,128)(2,1)S(1)}, u32[]{:S(2)}, u32[]{:S(2)}) collective-permute-start(bf16[384,128]{1,0:T(8,128)(2,1)} %param.9), channel_id=1, source_target_pairs={{0,1},{1,2},{2,3},{3,4},{4,5},{5,6},{6,7},{7,8},{8,9},{9,10},{10,1... | collective-permute-start | bytes 294920 | tf_op jit(solution)/shard_map/ppermute | solution.py:12
  5.9 1.3 %collective-permute-start.7 = (bf16[384,128]{1,0:T(8,128)(2,1)}, bf16[384,128]{1,0:T(8,128)(2,1)S(1)}, u32[]{:S(2)}, u32[]{:S(2)}) collective-permute-start(bf16[384,128]{1,0:T(8,128)(2,1)} %param.9), channel_id=1, source_target_pairs={{0,4},{1,5},{2,6},{3,7},{4,8},{5,9},{6,10},{7,11},{8,12},{9,13},{1... | collective-permute-start | bytes 294920 | tf_op jit(solution)/shard_map/ppermute | solution.py:12
  10.9 2.0 %fusion.99 = f32[384,384,8]{1,0,2:T(8,128)S(1)} fusion(bf16[384,128]{1,0:T(8,128)(2,1)} %param.8, bf16[384,1024]{1,0:T(8,128)(2,1)} %param.7), kind=kOutput, calls=%fused_computation.92 | convolution fusion | flops 301989888 | bytes 5603328 | tf_op jit(solution)/shard_map/qhd,kd->hqk/dot_general | solution.py:38
  15.1 1.7 %fusion.17 = bf16[8,384,384]{1,2,0:T(8,128)(2,1)S(1)} fusion(f32[384,384,8]{1,0,2:T(8,128)S(1)} %fusion.99, f32[8,384]{1,0:T(8,128)S(1)} %copy-done.7, f32[8,384]{1,0:T(8,128)S(1)} %copy-done.8, pred[384,384]{0,1:T(8,128)(4,1)S(1)} %get-tuple-element.20, bf16[384,128]{1,0:T(8,128)(2,1)S(1)} %copy-done.6, bf16[384,1024]{1,0:T(8,128)(2,1)S(1)} %copy-done), kind=kOutput, calls=%fused_computation.26 | convolution fusion | flops 309067776 | bytes 8134656 | tf_op jit(solution)/shard_map/qhd,kd->hqk/dot_general | solution.py:43
  21.3 5.0 %collective-permute-done.6 = bf16[384,128]{1,0:T(8,128)(2,1)S(1)} collective-permute-done((bf16[384,128]{1,0:T(8,128)(2,1)S(1)}, bf16[384,128]{1,0:T(8,128)(2,1)S(1)}, u32[]{:S(2)}, u32[]{:S(2)}) %collective-permute-start.6) | collective-permute-done | bytes 98336 | tf_op jit(solution)/shard_map/ppermute | solution.py:12
  26.3 2.9 %collective-permute-start = (bf16[384,128]{1,0:T(8,128)(2,1)S(1)}, bf16[384,128]{1,0:T(8,128)(2,1)S(1)}, u32[]{:S(2)}, u32[]{:S(2)}) collective-permute-start(bf16[384,128]{1,0:T(8,128)(2,1)S(1)} %copy-done.5), channel_id=1, source_target_pairs={{0,1},{1,2},{2,3},{3,4},{4,5},{5,6},{6,7},{7,8},{8,9},{9,10},{10,1... | collective-permute-start | bytes 294920 | tf_op jit(solution)/shard_map/ppermute | solution.py:12
  31.0 1.9 %collective-permute-start.2 = (bf16[384,128]{1,0:T(8,128)(2,1)S(1)}, bf16[384,128]{1,0:T(8,128)(2,1)S(1)}, u32[]{:S(2)}, u32[]{:S(2)}) collective-permute-start(bf16[384,128]{1,0:T(8,128)(2,1)S(1)} %copy-done.5), channel_id=1, source_target_pairs={{0,2},{1,3},{2,4},{3,5},{4,6},{5,7},{6,8},{7,9},{8,10},{9,11},{10,... | collective-permute-start | bytes 294920 | tf_op jit(solution)/shard_map/ppermute | solution.py:12
  32.9 1.7 %fusion.5 = bf16[8,384,384]{1,2,0:T(8,128)(2,1)S(1)} fusion(f32[384,384,8]{1,0,2:T(8,128)S(1)} %fusion.93, f32[8,384]{1,0:T(8,128)S(1)} %copy-done.7, f32[8,384]{1,0:T(8,128)S(1)} %copy-done.8, pred[384,384]{0,1:T(8,128)(4,1)S(1)} %get-tuple-element.18, bf16[384,128]{1,0:T(8,128)(2,1)S(1)} %collective-permute-done.5, bf16[384,1024]{1,0:T(8,128)(2,1)S(1)} %copy-done), kind=kOutput, calls=%fused_computation.8 | convolution fusion | flops 309067776 | bytes 8134656 | tf_op jit(solution)/shard_map/qhd,kd->hqk/dot_general | solution.py:43
  35.4 3.9 %collective-permute-done.2 = bf16[384,128]{1,0:T(8,128)(2,1)S(1)} collective-permute-done((bf16[384,128]{1,0:T(8,128)(2,1)S(1)}, bf16[384,128]{1,0:T(8,128)(2,1)S(1)}, u32[]{:S(2)}, u32[]{:S(2)}) %collective-permute-start.2) | collective-permute-done | bytes 98336 | tf_op jit(solution)/shard_map/ppermute | solution.py:12
  39.3 4.4 %collective-permute-start.10 = (bf16[384,128]{1,0:T(8,128)(2,1)S(1)}, bf16[384,128]{1,0:T(8,128)(2,1)S(1)}, u32[]{:S(2)}, u32[]{:S(2)}) collective-permute-start(bf16[384,128]{1,0:T(8,128)(2,1)S(1)} %fusion.73), channel_id=1, source_target_pairs={{3,0},{4,1},{5,2},{6,3},{7,4},{8,5},{9,6},{10,7},{11,8},{12,9},{13... | collective-permute-start | bytes 294920 | tf_op jit(solution)/shard_map/ppermute | solution.py:12
  45.6 4.5 %collective-permute-start.14 = (bf16[384,128]{1,0:T(8,128)(2,1)S(1)}, bf16[384,128]{1,0:T(8,128)(2,1)S(1)}, u32[]{:S(2)}, u32[]{:S(2)}) collective-permute-start(bf16[384,128]{1,0:T(8,128)(2,1)S(1)} %fusion.63), channel_id=1, source_target_pairs={{3,0},{4,1},{5,2},{6,3},{7,4},{8,5},{9,6},{10,7},{11,8},{12,9},{13... | collective-permute-start | bytes 294920 | tf_op jit(solution)/shard_map/ppermute | solution.py:12
  50.1 1.7 %fusion.1 = bf16[8,384,384]{1,2,0:T(8,128)(2,1)S(1)} fusion(f32[384,384,8]{1,0,2:T(8,128)S(1)} %fusion.91, f32[8,384]{1,0:T(8,128)S(1)} %copy-done.7, f32[8,384]{1,0:T(8,128)S(1)} %copy-done.8, pred[384,384]{0,1:T(8,128)(4,1)S(1)} %get-tuple-element.17, bf16[384,128]{1,0:T(8,128)(2,1)S(1)} %collective-permute-done.7, bf16[384,1024]{1,0:T(8,128)(2,1)S(1)} %copy-done), kind=kOutput, calls=%fused_computation.2 | convolution fusion | flops 309067776 | bytes 8134656 | tf_op jit(solution)/shard_map/qhd,kd->hqk/dot_general | solution.py:43
  52.6 3.5 %collective-permute-start.15 = (bf16[384,128]{1,0:T(8,128)(2,1)S(1)}, bf16[384,128]{1,0:T(8,128)(2,1)S(1)}, u32[]{:S(2)}, u32[]{:S(2)}) collective-permute-start(bf16[384,128]{1,0:T(8,128)(2,1)S(1)} %fusion.60), channel_id=1, source_target_pairs={{4,0},{5,1},{6,2},{7,3},{8,4},{9,5},{10,6},{11,7},{12,8},{13,9},{1... | collective-permute-start | bytes 294920 | tf_op jit(solution)/shard_map/ppermute | solution.py:12
  56.2 1.7 %fusion.9 = bf16[8,384,384]{1,2,0:T(8,128)(2,1)S(1)} fusion(f32[384,384,8]{1,0,2:T(8,128)S(1)} %fusion.95, f32[8,384]{1,0:T(8,128)S(1)} %copy-done.7, f32[8,384]{1,0:T(8,128)S(1)} %copy-done.8, pred[384,384]{0,1:T(8,128)(4,1)S(1)} %get-tuple-element.19, bf16[384,128]{1,0:T(8,128)(2,1)S(1)} %collective-permute-done.3, bf16[384,1024]{1,0:T(8,128)(2,1)S(1)} %copy-done), kind=kOutput, calls=%fused_computation.14 | convolution fusion | flops 309067776 | bytes 8134656 | tf_op jit(solution)/shard_map/qhd,kd->hqk/dot_general | solution.py:43
  58.7 5.1 %collective-permute-start.13 = (bf16[384,128]{1,0:T(8,128)(2,1)S(1)}, bf16[384,128]{1,0:T(8,128)(2,1)}, u32[]{:S(2)}, u32[]{:S(2)}) collective-permute-start(bf16[384,128]{1,0:T(8,128)(2,1)S(1)} %fusion.66), channel_id=1, source_target_pairs={{2,0},{3,1},{4,2},{5,3},{6,4},{7,5},{8,6},{9,7},{10,8},{11,9},{12,... | collective-permute-start | bytes 294920 | tf_op jit(solution)/shard_map/ppermute | solution.py:12
  64.5 1.6 %fusion.69 = bf16[384,128]{1,0:T(8,128)(2,1)} fusion(f32[384,384,8]{1,0,2:T(8,128)S(1)} %fusion.97, f32[8,384]{1,0:T(8,128)S(1)} %copy-done.8, pred[384,384]{0,1:T(8,128)(4,1)S(1)} %get-tuple-element.21, bf16[384,1024]{1,0:T(8,128)(2,1)S(1)} %copy-done), kind=kOutput, calls=%fused_computation.64 | convolution fusion | flops 306757632 | bytes 5763072 | tf_op jit(solution)/shard_map/hqk,qhd->kd/dot_general | solution.py:55
  66.1 1.7 %fusion.13 = bf16[8,384,384]{1,2,0:T(8,128)(2,1)S(1)} fusion(f32[384,384,8]{1,0,2:T(8,128)S(1)} %fusion.97, f32[8,384]{1,0:T(8,128)S(1)} %copy-done.7, f32[8,384]{1,0:T(8,128)S(1)} %copy-done.8, pred[384,384]{0,1:T(8,128)(4,1)S(1)} %get-tuple-element.21, bf16[384,128]{1,0:T(8,128)(2,1)S(1)} %collective-permute-done.1, bf16[384,1024]{1,0:T(8,128)(2,1)S(1)} %copy-done), kind=kOutput, calls=%fused_computation.20 | convolution fusion | flops 309067776 | bytes 8134656 | tf_op jit(solution)/shard_map/qhd,kd->hqk/dot_general | solution.py:43
  68.6 2.9 %collective-permute-start.12 = (bf16[384,128]{1,0:T(8,128)(2,1)}, bf16[384,128]{1,0:T(8,128)(2,1)}, u32[]{:S(2)}, u32[]{:S(2)}) collective-permute-start(bf16[384,128]{1,0:T(8,128)(2,1)} %fusion.69), channel_id=1, source_target_pairs={{1,0},{2,1},{3,2},{4,3},{5,4},{6,5},{7,6},{8,7},{9,8},{10,9},{11,1... | collective-permute-start | bytes 294920 | tf_op jit(solution)/shard_map/ppermute | solution.py:12
  75.6 1.8 %collective-permute-start.11 = (bf16[384,128]{1,0:T(8,128)(2,1)S(1)}, bf16[384,128]{1,0:T(8,128)(2,1)S(1)}, u32[]{:S(2)}, u32[]{:S(2)}) collective-permute-start(bf16[384,128]{1,0:T(8,128)(2,1)S(1)} %fusion.72), channel_id=1, source_target_pairs={{4,0},{5,1},{6,2},{7,3},{8,4},{9,5},{10,6},{11,7},{12,8},{13,9},{1... | collective-permute-start | bytes 294920 | tf_op jit(solution)/shard_map/ppermute | solution.py:12
  77.4 2.3 %collective-permute-start.9 = (bf16[384,128]{1,0:T(8,128)(2,1)S(1)}, bf16[384,128]{1,0:T(8,128)(2,1)S(1)}, u32[]{:S(2)}, u32[]{:S(2)}) collective-permute-start(bf16[384,128]{1,0:T(8,128)(2,1)S(1)} %fusion.74), channel_id=1, source_target_pairs={{2,0},{3,1},{4,2},{5,3},{6,4},{7,5},{8,6},{9,7},{10,8},{11,9},{12,... | collective-permute-start | bytes 294920 | tf_op jit(solution)/shard_map/ppermute | solution.py:12
  79.7 4.1 %collective-permute-start.8 = (bf16[384,128]{1,0:T(8,128)(2,1)S(1)}, bf16[384,128]{1,0:T(8,128)(2,1)S(1)}, u32[]{:S(2)}, u32[]{:S(2)}) collective-permute-start(bf16[384,128]{1,0:T(8,128)(2,1)S(1)} %fusion.75), channel_id=1, source_target_pairs={{1,0},{2,1},{3,2},{4,3},{5,4},{6,5},{7,6},{8,7},{9,8},{10,9},{11,1... | collective-permute-start | bytes 294920 | tf_op jit(solution)/shard_map/ppermute | solution.py:12
  83.8 4.1 %add_convert_fusion = bf16[384,128]{1,0:T(8,128)(2,1)} fusion(bf16[384,128]{1,0:T(8,128)(2,1)S(1)} %collective-permute-done.15, bf16[384,128]{1,0:T(8,128)(2,1)S(1)} %collective-permute-done.14, bf16[384,128]{1,0:T(8,128)(2,1)} %collective-permute-done.13, bf16[384,128]{1,0:T(8,128)(2,1)} %collective-permute-done.12, f32[384,384,8]{1,0,2:T(8,128)} %copy-done.2, ...), kind=kOutput, calls=%fused_computation.99 | convolution fusion | flops 307150848 | bytes 6156288 | tf_op jit(solution)/shard_map/hqk,qhd->kd/dot_general | solution.py:55
  87.9 1.4 %add_convert_fusion.1 = bf16[384,128]{1,0:T(8,128)(2,1)} fusion(bf16[384,128]{1,0:T(8,128)(2,1)S(1)} %collective-permute-done.11, bf16[384,128]{1,0:T(8,128)(2,1)S(1)} %collective-permute-done.10, bf16[384,128]{1,0:T(8,128)(2,1)S(1)} %collective-permute-done.9, bf16[384,128]{1,0:T(8,128)(2,1)S(1)} %collective-permute-done.8, ...), kind=kOutput, calls=%fused_computation.100 | convolution fusion | flops 302481408 | bytes 3637248 | tf_op jit(solution)/shard_map/hqk,qhd->kd/dot_general | solution.py:52
  (64 shorter events, 21.7 us)
Async XLA Ops:
  0.6 14.4 %copy-start = (bf16[384,1024]{1,0:T(8,128)(2,1)S(1)}, bf16[384,1024]{1,0:T(8,128)(2,1)}, u32[]{:S(2)}) copy-start(bf16[384,1024]{1,0:T(8,128)(2,1)} %param.10) | copy-start | bytes 2359300
  0.6 14.4 %copy-start.6 = (bf16[384,128]{1,0:T(8,128)(2,1)S(1)}, bf16[384,128]{1,0:T(8,128)(2,1)}, u32[]{:S(2)}) copy-start(bf16[384,128]{1,0:T(8,128)(2,1)} %param.9) | copy-start | bytes 294916
  0.7 14.4 %copy-start.8 = (f32[8,384]{1,0:T(8,128)S(1)}, f32[8,384]{1,0:T(8,128)}, u32[]{:S(2)}) copy-start(f32[8,384]{1,0:T(8,128)} %param.11) | copy-start | bytes 36868
  0.7 14.4 %copy-start.7 = (f32[8,384]{1,0:T(8,128)S(1)}, f32[8,384]{1,0:T(8,128)}, u32[]{:S(2)}) copy-start(f32[8,384]{1,0:T(8,128)} %param.12) | copy-start | bytes 36868
  0.7 51.9 %collective-permute-start.3 = (bf16[384,128]{1,0:T(8,128)(2,1)}, bf16[384,128]{1,0:T(8,128)(2,1)S(1)}, u32[]{:S(2)}, u32[]{:S(2)}) collective-permute-start(bf16[384,128]{1,0:T(8,128)(2,1)} %param.9), channel_id=1, source_target_pairs={{0,2},{1,3},{2,4},{3,5},{4,6},{5,7},{6,8},{7,9},{8,10},{9,11},{10,... | collective-permute-start | bytes 294920 | tf_op jit(solution)/shard_map/ppermute | solution.py:12
  3.9 62.2 %collective-permute-start.1 = (bf16[384,128]{1,0:T(8,128)(2,1)}, bf16[384,128]{1,0:T(8,128)(2,1)S(1)}, u32[]{:S(2)}, u32[]{:S(2)}) collective-permute-start(bf16[384,128]{1,0:T(8,128)(2,1)} %param.9), channel_id=1, source_target_pairs={{0,1},{1,2},{2,3},{3,4},{4,5},{5,6},{6,7},{7,8},{8,9},{9,10},{10,1... | collective-permute-start | bytes 294920 | tf_op jit(solution)/shard_map/ppermute | solution.py:12
  5.9 39.7 %collective-permute-start.7 = (bf16[384,128]{1,0:T(8,128)(2,1)}, bf16[384,128]{1,0:T(8,128)(2,1)S(1)}, u32[]{:S(2)}, u32[]{:S(2)}) collective-permute-start(bf16[384,128]{1,0:T(8,128)(2,1)} %param.9), channel_id=1, source_target_pairs={{0,4},{1,5},{2,6},{3,7},{4,8},{5,9},{6,10},{7,11},{8,12},{9,13},{1... | collective-permute-start | bytes 294920 | tf_op jit(solution)/shard_map/ppermute | solution.py:12
  7.2 23.8 %collective-permute-start.5 = (bf16[384,128]{1,0:T(8,128)(2,1)}, bf16[384,128]{1,0:T(8,128)(2,1)S(1)}, u32[]{:S(2)}, u32[]{:S(2)}) collective-permute-start(bf16[384,128]{1,0:T(8,128)(2,1)} %param.9), channel_id=1, source_target_pairs={{0,3},{1,4},{2,5},{3,6},{4,7},{5,8},{6,9},{7,10},{8,11},{9,12},{10... | collective-permute-start | bytes 294920 | tf_op jit(solution)/shard_map/ppermute | solution.py:12
  8.5 8.9 %collective-permute-start.4 = (bf16[384,128]{1,0:T(8,128)(2,1)}, bf16[384,128]{1,0:T(8,128)(2,1)S(1)}, u32[]{:S(2)}, u32[]{:S(2)}) collective-permute-start(bf16[384,128]{1,0:T(8,128)(2,1)} %param.8), channel_id=1, source_target_pairs={{0,3},{1,4},{2,5},{3,6},{4,7},{5,8},{6,9},{7,10},{8,11},{9,12},{10... | collective-permute-start | bytes 294920 | tf_op jit(solution)/shard_map/ppermute | solution.py:12
  12.9 2.1 %copy-start.2 = (f32[384,384,8]{1,0,2:T(8,128)}, f32[384,384,8]{1,0,2:T(8,128)S(1)}, u32[]{:S(2)}) copy-start(f32[384,384,8]{1,0,2:T(8,128)S(1)} %fusion.99) | copy-start | bytes 14155780
  15.0 1.7 %copy-start.5 = (bf16[384,128]{1,0:T(8,128)(2,1)S(1)}, bf16[384,128]{1,0:T(8,128)(2,1)}, u32[]{:S(2)}) copy-start(bf16[384,128]{1,0:T(8,128)(2,1)} %param.8) | copy-start | bytes 294916
  15.0 4.5 %copy-start.1 = (bf16[384,1024]{1,0:T(8,128)(2,1)S(1)}, bf16[384,1024]{1,0:T(8,128)(2,1)}, u32[]{:S(2)}) copy-start(bf16[384,1024]{1,0:T(8,128)(2,1)} %param.7) | copy-start | bytes 2359300
  18.2 8.0 %collective-permute-start.6 = (bf16[384,128]{1,0:T(8,128)(2,1)S(1)}, bf16[384,128]{1,0:T(8,128)(2,1)S(1)}, u32[]{:S(2)}, u32[]{:S(2)}) collective-permute-start(bf16[384,128]{1,0:T(8,128)(2,1)S(1)} %copy-done.5), channel_id=1, source_target_pairs={{0,4},{1,5},{2,6},{3,7},{4,8},{5,9},{6,10},{7,11},{8,12},{9,13},{1... | collective-permute-start | bytes 294920 | tf_op jit(solution)/shard_map/ppermute | solution.py:12
  26.3 32.4 %collective-permute-start = (bf16[384,128]{1,0:T(8,128)(2,1)S(1)}, bf16[384,128]{1,0:T(8,128)(2,1)S(1)}, u32[]{:S(2)}, u32[]{:S(2)}) collective-permute-start(bf16[384,128]{1,0:T(8,128)(2,1)S(1)} %copy-done.5), channel_id=1, source_target_pairs={{0,1},{1,2},{2,3},{3,4},{4,5},{5,6},{6,7},{7,8},{8,9},{9,10},{10,1... | collective-permute-start | bytes 294920 | tf_op jit(solution)/shard_map/ppermute | solution.py:12
  31.0 8.3 %collective-permute-start.2 = (bf16[384,128]{1,0:T(8,128)(2,1)S(1)}, bf16[384,128]{1,0:T(8,128)(2,1)S(1)}, u32[]{:S(2)}, u32[]{:S(2)}) collective-permute-start(bf16[384,128]{1,0:T(8,128)(2,1)S(1)} %copy-done.5), channel_id=1, source_target_pairs={{0,2},{1,3},{2,4},{3,5},{4,6},{5,7},{6,8},{7,9},{8,10},{9,11},{10,... | collective-permute-start | bytes 294920 | tf_op jit(solution)/shard_map/ppermute | solution.py:12
  39.3 48.5 %collective-permute-start.10 = (bf16[384,128]{1,0:T(8,128)(2,1)S(1)}, bf16[384,128]{1,0:T(8,128)(2,1)S(1)}, u32[]{:S(2)}, u32[]{:S(2)}) collective-permute-start(bf16[384,128]{1,0:T(8,128)(2,1)S(1)} %fusion.73), channel_id=1, source_target_pairs={{3,0},{4,1},{5,2},{6,3},{7,4},{8,5},{9,6},{10,7},{11,8},{12,9},{13... | collective-permute-start | bytes 294920 | tf_op jit(solution)/shard_map/ppermute | solution.py:12
  45.6 30.0 %collective-permute-start.14 = (bf16[384,128]{1,0:T(8,128)(2,1)S(1)}, bf16[384,128]{1,0:T(8,128)(2,1)S(1)}, u32[]{:S(2)}, u32[]{:S(2)}) collective-permute-start(bf16[384,128]{1,0:T(8,128)(2,1)S(1)} %fusion.63), channel_id=1, source_target_pairs={{3,0},{4,1},{5,2},{6,3},{7,4},{8,5},{9,6},{10,7},{11,8},{12,9},{13... | collective-permute-start | bytes 294920 | tf_op jit(solution)/shard_map/ppermute | solution.py:12
  52.6 24.7 %collective-permute-start.15 = (bf16[384,128]{1,0:T(8,128)(2,1)S(1)}, bf16[384,128]{1,0:T(8,128)(2,1)S(1)}, u32[]{:S(2)}, u32[]{:S(2)}) collective-permute-start(bf16[384,128]{1,0:T(8,128)(2,1)S(1)} %fusion.60), channel_id=1, source_target_pairs={{4,0},{5,1},{6,2},{7,3},{8,4},{9,5},{10,6},{11,7},{12,8},{13,9},{1... | collective-permute-start | bytes 294920 | tf_op jit(solution)/shard_map/ppermute | solution.py:12
  58.7 21.0 %collective-permute-start.13 = (bf16[384,128]{1,0:T(8,128)(2,1)S(1)}, bf16[384,128]{1,0:T(8,128)(2,1)}, u32[]{:S(2)}, u32[]{:S(2)}) collective-permute-start(bf16[384,128]{1,0:T(8,128)(2,1)S(1)} %fusion.66), channel_id=1, source_target_pairs={{2,0},{3,1},{4,2},{5,3},{6,4},{7,5},{8,6},{9,7},{10,8},{11,9},{12,... | collective-permute-start | bytes 294920 | tf_op jit(solution)/shard_map/ppermute | solution.py:12
  68.6 15.1 %collective-permute-start.12 = (bf16[384,128]{1,0:T(8,128)(2,1)}, bf16[384,128]{1,0:T(8,128)(2,1)}, u32[]{:S(2)}, u32[]{:S(2)}) collective-permute-start(bf16[384,128]{1,0:T(8,128)(2,1)} %fusion.69), channel_id=1, source_target_pairs={{1,0},{2,1},{3,2},{4,3},{5,4},{6,5},{7,6},{8,7},{9,8},{10,9},{11,1... | collective-permute-start | bytes 294920 | tf_op jit(solution)/shard_map/ppermute | solution.py:12
  75.6 12.3 %copy-start.4 = (bf16[8,384,384]{1,2,0:T(8,128)(2,1)S(1)}, bf16[8,384,384]{1,2,0:T(8,128)(2,1)}, u32[]{:S(2)}) copy-start(bf16[8,384,384]{1,2,0:T(8,128)(2,1)} %copy-done.3) | copy-start | bytes 7077892
  75.6 12.3 %collective-permute-start.11 = (bf16[384,128]{1,0:T(8,128)(2,1)S(1)}, bf16[384,128]{1,0:T(8,128)(2,1)S(1)}, u32[]{:S(2)}, u32[]{:S(2)}) collective-permute-start(bf16[384,128]{1,0:T(8,128)(2,1)S(1)} %fusion.72), channel_id=1, source_target_pairs={{4,0},{5,1},{6,2},{7,3},{8,4},{9,5},{10,6},{11,7},{12,8},{13,9},{1... | collective-permute-start | bytes 294920 | tf_op jit(solution)/shard_map/ppermute | solution.py:12
  77.4 10.5 %collective-permute-start.9 = (bf16[384,128]{1,0:T(8,128)(2,1)S(1)}, bf16[384,128]{1,0:T(8,128)(2,1)S(1)}, u32[]{:S(2)}, u32[]{:S(2)}) collective-permute-start(bf16[384,128]{1,0:T(8,128)(2,1)S(1)} %fusion.74), channel_id=1, source_target_pairs={{2,0},{3,1},{4,2},{5,3},{6,4},{7,5},{8,6},{9,7},{10,8},{11,9},{12,... | collective-permute-start | bytes 294920 | tf_op jit(solution)/shard_map/ppermute | solution.py:12
  79.7 8.2 %collective-permute-start.8 = (bf16[384,128]{1,0:T(8,128)(2,1)S(1)}, bf16[384,128]{1,0:T(8,128)(2,1)S(1)}, u32[]{:S(2)}, u32[]{:S(2)}) collective-permute-start(bf16[384,128]{1,0:T(8,128)(2,1)S(1)} %fusion.75), channel_id=1, source_target_pairs={{1,0},{2,1},{3,2},{4,3},{5,4},{6,5},{7,6},{8,7},{9,8},{10,9},{11,1... | collective-permute-start | bytes 294920 | tf_op jit(solution)/shard_map/ppermute | solution.py:12
  (1 other events, 1.4 us)
where the time goes:
time: 89.9 us; the launch traced here: 89.3 us
  starting transfers between devices  43.8 us (49%)
  matrix products  30.2 us (34%)
  waiting for transfers between devices  8.93 us (10%)
  local copies, waits for them, and re-layouts  4 us (4%)
  other arithmetic  1.2 us (1%)
  between operations  1.13 us (1%)
    ppermute x16, starting transfers between devices, from_behind(): return lax.ppermute(array, axis, pairs)  43.8 us
    ppermute x16, waiting for transfers between devices, from_behind(): return lax.ppermute(array, axis, pairs)  8.93 us
    dot_general x5, matrix products, block_grads(): jnp.einsum('hqk,qhd->kd', probs_half, grad_heads, preferred_element_type=...  8.65 us
    dot_general x5, matrix products, block_grads(): jnp.einsum('qhd,kd->hqk', grad_heads, value_block, preferred_element_type...  8.52 us
    dot_general x5, matrix products, block_grads(): jnp.einsum('qhd,kd->hqk', query_heads, key_block, preferred_element_type=...  5.08 us
    dot_general x5, matrix products, block_grads(): jnp.einsum('hqk,qhd->kd', dscores_half, query_heads, preferred_element_ty...  4.56 us
    dot_general x5, matrix products, block_grads(): jnp.einsum('hqk,kd->qhd', dscores_half, key_block, preferred_element_type...  3.42 us
    unnamed x19, local copies, waits for them, and re-layouts  3.25 us
  transfers between devices with their start and end apart: 16, of which 2 were waited for; matrix products, arithmetic and copies ran while one was open for 36% of the time, Pallas kernels for 0%

commit v1 on v0

v1 whole, which is shorter than its diff:
```python
import functools
import math

import jax
import jax.numpy as jnp
from jax import lax
from jax.experimental import pallas as pl
from jax.experimental.pallas import tpu as pltpu
from jax.sharding import PartitionSpec as P

REACH = 4
LANES = 128
LOG2E = math.log2(math.e)
MESH = pl.DeviceIdType.MESH


def dot(a, b):
    return jnp.dot(a, b, preferred_element_type=jnp.float32)


def dot_nt(a, b):
    return lax.dot_general(a, b, (((1,), (1,)), ((), ())), preferred_element_type=jnp.float32)


def kernel(
    count,
    per_seq,
    lens_ref,
    q_hbm,
    g_hbm,
    k_ref,
    v_ref,
    lse_ref,
    delta_ref,
    dq_ref,
    dk_ref,
    dv_ref,
    q,
    g,
    kbuf,
    vbuf,
    k_t,
    bias,
    lse2,
    dq_t,
    own_k,
    own_v,
    acc_k,
    acc_v,
    out_k,
    out_v,
    in_k,
    in_v,
    load_sem,
    kv_send,
    kv_recv,
    gr_send,
    gr_recv,
):
    rows, head = k_ref.shape
    heads = q.shape[1] // head
    scale = head**-0.5
    me = lax.axis_index("seq") * per_seq + lax.axis_index("rep")

    def device(index):
        return (lax.div(index, per_seq), lax.rem(index, per_seq))

    load_q = pltpu.make_async_copy(q_hbm, q, load_sem.at[0])
    load_g = pltpu.make_async_copy(g_hbm, g, load_sem.at[1])
    load_q.start()
    load_g.start()

    barrier = pltpu.get_barrier_semaphore()
    for d in range(1, REACH + 1):

        @pl.when(me + d < count)
        def _():
            pl.semaphore_signal(barrier, inc=1, device_id=device(me + d), device_id_type=MESH)

        @pl.when(me >= d)
        def _():
            pl.semaphore_signal(barrier, inc=1, device_id=device(me - d), device_id_type=MESH)

    pl.semaphore_wait(barrier, jnp.minimum(me, REACH) + jnp.minimum(count - 1 - me, REACH))

    def kv_copies(d):
        return [
            pltpu.make_async_remote_copy(
                src_ref=src,
                dst_ref=dst.at[d - 1],
                send_sem=kv_send.at[n, d - 1],
                recv_sem=kv_recv.at[n, d - 1],
                device_id=device(me + d),
                device_id_type=MESH,
            )
            for n, (src, dst) in enumerate(((k_ref, kbuf), (v_ref, vbuf)))
        ]

    def grad_copies(d):
        return [
            pltpu.make_async_remote_copy(
                src_ref=src.at[d - 1],
                dst_ref=dst.at[d - 1],
                send_sem=gr_send.at[n, d - 1],
                recv_sem=gr_recv.at[n, d - 1],
                device_id=device(me - d),
                device_id_type=MESH,
            )
            for n, (src, dst) in enumerate(((out_k, in_k), (out_v, in_v)))
        ]

    for d in range(1, REACH + 1):

        @pl.when(me + d < count)
        def _():
            for copy in kv_copies(d):
                copy.start()

    t_pos = me * rows + lax.broadcasted_iota(jnp.int32, (1, rows), 1)

    def next_doc(j, carry):
        end, start = carry
        end = end + lens_ref[j]
        return end, jnp.where(end <= t_pos, end, start)

    _, start = lax.fori_loop(
        0, lens_ref.shape[0], next_doc, (jnp.int32(0), jnp.zeros((1, rows), jnp.int32))
    )
    lse2[...] = lse_ref[...] * LOG2E

    def set_bias(d):
        u_pos = (me - d) * rows + lax.broadcasted_iota(jnp.int32, (rows, rows), 0)
        bias[...] = jnp.where((u_pos >= start) & (u_pos <= t_pos), 0.0, -1e30)

    def columns(h):
        return pl.ds(pl.multiple_of(h * head, head), head)

    def grads(h, k_tile, v_tile, bias_tile, q_tile, g_tile, lse_tile, delta_tile):
        p = jnp.exp2(dot_nt(k_tile, q_tile) * (scale * LOG2E) + (bias_tile - lse_tile))
        ds = (p * (dot_nt(v_tile, g_tile) - delta_tile)).astype(jnp.bfloat16)
        return dot(ds, q_tile), dot(p.astype(jnp.bfloat16), g_tile), ds

    set_bias(0)
    k_t[...] = k_ref[...].astype(jnp.float32).T.astype(jnp.bfloat16)
    own_k[...] = jnp.zeros_like(own_k)
    own_v[...] = jnp.zeros_like(own_v)
    load_q.wait()
    load_g.wait()
    tile = LANES if rows % LANES == 0 else rows

    def own_head(h, carry):
        dq_t[columns(h), :] = jnp.zeros((head, rows), jnp.float32)
        for low in range(0, rows, tile):
            u = slice(low, low + tile)
            dk, dv, ds = grads(
                h,
                k_ref[u, :],
                v_ref[u, :],
                bias[u, low:],
                q[low:, columns(h)],
                g[low:, columns(h)],
                lse2[pl.ds(h, 1), :][:, low:],
                delta_ref[pl.ds(h, 1), :][:, low:],
            )
            own_k[u, :] += dk
            own_v[u, :] += dv
            dq_t[columns(h), low:] += dot(k_t[:, u], ds)
        return carry

    lax.fori_loop(0, heads, own_head, 0)

    def cross(d, carry):
        @pl.when(me >= d)
        def _():
            for copy in kv_copies(d):
                copy.wait_recv()
            set_bias(d)
            k_t[...] = kbuf[d - 1].astype(jnp.float32).T.astype(jnp.bfloat16)
            acc_k[...] = jnp.zeros_like(acc_k)
            acc_v[...] = jnp.zeros_like(acc_v)

            def one_head(h, inner):
                dk, dv, ds = grads(
                    h,
                    kbuf[d - 1],
                    vbuf[d - 1],
                    bias[...],
                    q[:, columns(h)],
                    g[:, columns(h)],
                    lse2[pl.ds(h, 1), :],
                    delta_ref[pl.ds(h, 1), :],
                )
                acc_k[...] += dk
                acc_v[...] += dv
                dq_t[columns(h), :] += dot(k_t[...], ds)
                return inner

            lax.fori_loop(0, heads, one_head, 0)
            out_k[d - 1] = (acc_k[...] * scale).astype(jnp.bfloat16)
            out_v[d - 1] = acc_v[...].astype(jnp.bfloat16)
            for copy in grad_copies(d):
                copy.start()

        return carry

    lax.fori_loop(1, REACH + 1, cross, 0)

    for h in range(heads):
        c = slice(h * head, (h + 1) * head)
        dq_ref[:, c] = (dq_t[c, :] * scale).T.astype(jnp.bfloat16)

    own_k[...] = own_k[...] * scale
    for d in range(1, REACH + 1):

        @pl.when(me + d < count)
        def _():
            for copy in grad_copies(d):
                copy.wait_recv()
            own_k[...] += in_k[d - 1].astype(jnp.float32)
            own_v[...] += in_v[d - 1].astype(jnp.float32)
            for copy in kv_copies(d):
                copy.wait_send()

        @pl.when(me >= d)
        def _():
            for copy in grad_copies(d):
                copy.wait_send()

    dk_ref[...] = own_k[...].astype(jnp.bfloat16)
    dv_ref[...] = own_v[...].astype(jnp.bfloat16)


def shards(count, per_seq, query_rows, key_rows, value_rows, out_grad, logsumexp, row_delta, doc_lengths):
    rows, head = key_rows.shape
    wide = query_rows.shape
    half, full = jnp.bfloat16, jnp.float32
    vmem = pl.BlockSpec(memory_space=pltpu.VMEM)
    hbm = pl.BlockSpec(memory_space=pl.ANY)
    return pl.pallas_call(
        functools.partial(kernel, count, per_seq),
        out_shape=(
            jax.ShapeDtypeStruct(wide, half),
            jax.ShapeDtypeStruct((rows, head), half),
            jax.ShapeDtypeStruct((rows, head), half),
        ),
        in_specs=[pl.BlockSpec(memory_space=pltpu.SMEM), hbm, hbm, vmem, vmem, vmem, vmem],
        out_specs=(vmem, vmem, vmem),
        scratch_shapes=[
            pltpu.VMEM(wide, half),
            pltpu.VMEM(wide, half),
            pltpu.VMEM((REACH, rows, head), half),
            pltpu.VMEM((REACH, rows, head), half),
            pltpu.VMEM((head, rows), half),
            pltpu.VMEM((rows, rows), full),
            pltpu.VMEM(logsumexp.shape, full),
            pltpu.VMEM((wide[1], rows), full),
            pltpu.VMEM((rows, head), full),
            pltpu.VMEM((rows, head), full),
            pltpu.VMEM((rows, head), full),
            pltpu.VMEM((rows, head), full),
            pltpu.VMEM((REACH, rows, head), half),
            pltpu.VMEM((REACH, rows, head), half),
            pltpu.VMEM((REACH, rows, head), half),
            pltpu.VMEM((REACH, rows, head), half),
            pltpu.SemaphoreType.DMA((2,)),
            pltpu.SemaphoreType.DMA((2, REACH)),
            pltpu.SemaphoreType.DMA((2, REACH)),
            pltpu.SemaphoreType.DMA((2, REACH)),
            pltpu.SemaphoreType.DMA((2, REACH)),
        ],
        compiler_params=pltpu.CompilerParams(collective_id=0, has_side_effects=True),
    )(doc_lengths, query_rows, out_grad, key_rows, value_rows, logsumexp, row_delta)


def solution(mesh):
    both = ("seq", "rep")
    count = mesh.shape["seq"] * mesh.shape["rep"]
    return jax.shard_map(
        functools.partial(shards, count, mesh.shape["rep"]),
        mesh=mesh,
        in_specs=(
            P(both, None),
            P(both, None),
            P(both, None),
            P(both, None),
            P(None, both),
            P(None, both),
            P(),
        ),
        out_specs=(P(both, None), P(both, None), P(both, None)),
        check_vma=False,
    )
```

time: 89.9 us -> 47.2 us (0.53)
  the two profiles are of different devices: /device:TPU:29 before, /device:TPU:7 now
where the time goes in v1:
time: 47.2 us; the launch traced here: 46.8 us
  Pallas kernels  42.4 us (90%)
  local copies, waits for them, and re-layouts  3.67 us (8%)
  between operations  0.65 us (1%)
    pallas_call x1, Pallas kernels, shards(): pl.pallas_call(functools.partial(kernel, count, per_seq), out_shape=(jax....  42.4 us
    unnamed x7, local copies, waits for them, and re-layouts  3.67 us

profile of v1, /device:TPU:7, one launch (start us, length us, event | category | flops | bytes accessed | tf_op | source)
XLA Modules:
  0.0 46.8 jit_solution(17957038460553929626)
XLA Ops:
  0.6 42.4 %shard_map.94 = (bf16[384,1024]{1,0:T(8,128)(2,1)}, bf16[384,128]{1,0:T(8,128)(2,1)}, bf16[384,128]{1,0:T(8,128)(2,1)}) custom-call(s32[31]{0:T(128)} %lens_ref.1, bf16[384,1024]{1,0:T(8,128)(2,1)} %q_hbm.1, bf16[384,1024]{1,0:T(8,128)(2,1)} %g_hbm.1, bf16[384,128]{1,0:T(8,128)(2,1)} %k_ref.1, bf16[384,128]{1,0:T(8,128)(2,1)} %v_ref.1, f32[8,384]{1,0:T(8,128)} %lse_ref.1, ...), custom_call_target="tpu_custom_call" | custom-call | tf_op jit(solution)/shard_map/pallas_call | solution.py:239
  43.1 0.0 copy-start.1
  43.1 2.1 %copy.13 = bf16[384,1024]{1,0:T(8,128)(2,1)} copy(bf16[384,1024]{1,0:T(8,128)(2,1)} %get-tuple-element.6) | data formatting | bytes 1572864
  45.2 0.0 copy-done.1
  45.2 0.0 copy-start
  45.2 0.6 %copy.14 = bf16[384,128]{1,0:T(8,128)(2,1)} copy(bf16[384,128]{1,0:T(8,128)(2,1)S(1)} %copy-done.1) | data formatting | bytes 196608
  45.8 0.3 copy-done
  46.1 0.6 %copy.15 = bf16[384,128]{1,0:T(8,128)(2,1)} copy(bf16[384,128]{1,0:T(8,128)(2,1)S(1)} %copy-done) | data formatting | bytes 196608
Async XLA Ops:
  43.1 2.1 %copy-start.1 = (bf16[384,128]{1,0:T(8,128)(2,1)S(1)}, bf16[384,128]{1,0:T(8,128)(2,1)}, u32[]{:S(2)}) copy-start(bf16[384,128]{1,0:T(8,128)(2,1)} %get-tuple-element.7) | copy-start | bytes 294916
  45.2 0.9 %copy-start = (bf16[384,128]{1,0:T(8,128)(2,1)S(1)}, bf16[384,128]{1,0:T(8,128)(2,1)}, u32[]{:S(2)}) copy-start(bf16[384,128]{1,0:T(8,128)(2,1)} %get-tuple-element.8) | copy-start | bytes 294916

commit v2 on v1

--- a/solution.py
+++ b/solution.py
@@ -10,6 +10,7 @@
 
 REACH = 4
 LANES = 128
+UNROLL = 2
 LOG2E = math.log2(math.e)
 MESH = pl.DeviceIdType.MESH
 
@@ -58,17 +59,25 @@
     gr_recv,
 ):
     rows, head = k_ref.shape
-    heads = q.shape[1] // head
+    heads = q_hbm.shape[1] // head
+    pack = 2 if heads % 2 == 0 else 1
     scale = head**-0.5
     me = lax.axis_index("seq") * per_seq + lax.axis_index("rep")
 
     def device(index):
         return (lax.div(index, per_seq), lax.rem(index, per_seq))
 
-    load_q = pltpu.make_async_copy(q_hbm, q, load_sem.at[0])
-    load_g = pltpu.make_async_copy(g_hbm, g, load_sem.at[1])
-    load_q.start()
-    load_g.start()
+    loads = [
+        pltpu.make_async_copy(
+            src.at[:, h * head : (h + 1) * head],
+            dst.at[h * rows : (h + 1) * rows, :],
+            load_sem.at[n, h],
+        )
+        for h in range(heads)
+        for n, (src, dst) in enumerate(((q_hbm, q), (g_hbm, g)))
+    ]
+    for copy in loads:
+        copy.start()
 
     barrier = pltpu.get_barrier_semaphore()
     for d in range(1, REACH + 1):
@@ -83,18 +92,39 @@
 
     pl.semaphore_wait(barrier, jnp.minimum(me, REACH) + jnp.minimum(count - 1 - me, REACH))
 
-    def kv_copies(d):
+    core = lax.rem(me, 2)
+    partner = me + 1 - 2 * core
+
+    def kv_copies(sources, d, target, order):
         return [
             pltpu.make_async_remote_copy(
                 src_ref=src,
                 dst_ref=dst.at[d - 1],
-                send_sem=kv_send.at[n, d - 1],
+                send_sem=kv_send.at[n, order],
                 recv_sem=kv_recv.at[n, d - 1],
-                device_id=device(me + d),
+                device_id=device(target),
                 device_id_type=MESH,
             )
-            for n, (src, dst) in enumerate(((k_ref, kbuf), (v_ref, vbuf)))
+            for n, (src, dst) in enumerate(zip(sources, (kbuf, vbuf)))
         ]
+
+    own = (k_ref, v_ref)
+    routes = [
+        (me + 2 < count, kv_copies(own, 2, me + 2, 0)),
+        (me + 4 < count, kv_copies(own, 4, me + 4, 1)),
+        (core == 0, kv_copies(own, 1, partner, 2)),
+        ((core == 0) & (me >= 2), kv_copies((kbuf.at[1], vbuf.at[1]), 3, partner, 3)),
+        ((core == 1) & (me >= 2), kv_copies((kbuf.at[1], vbuf.at[1]), 1, partner, 3)),
+        ((core == 1) & (me >= 4), kv_copies((kbuf.at[3], vbuf.at[3]), 3, partner, 4)),
+    ]
+
+    def send(numbers):
+        for number in numbers:
+
+            @pl.when(routes[number][0])
+            def _():
+                for copy in routes[number][1]:
+                    copy.start()
 
     def grad_copies(d):
         return [
@@ -109,12 +139,7 @@
             for n, (src, dst) in enumerate(((out_k, in_k), (out_v, in_v)))
         ]
 
-    for d in range(1, REACH + 1):
-
-        @pl.when(me + d < count)
-        def _():
-            for copy in kv_copies(d):
-                copy.start()
+    send((0, 1, 2))
 
     t_pos = me * rows + lax.broadcasted_iota(jnp.int32, (1, rows), 1)
 
@@ -135,7 +160,13 @@
     def columns(h):
         return pl.ds(pl.multiple_of(h * head, head), head)
 
-    def grads(h, k_tile, v_tile, bias_tile, q_tile, g_tile, lse_tile, delta_tile):
+    def stacked(h):
+        return pl.ds(pl.multiple_of(h * rows, rows), pack * rows)
+
+    def head_rows(ref, h):
+        return jnp.concatenate([ref[pl.ds(h + n, 1), :] for n in range(pack)], axis=1)
+
+    def grads(k_tile, v_tile, bias_tile, q_tile, g_tile, lse_tile, delta_tile):
         p = jnp.exp2(dot_nt(k_tile, q_tile) * (scale * LOG2E) + (bias_tile - lse_tile))
         ds = (p * (dot_nt(v_tile, g_tile) - delta_tile)).astype(jnp.bfloat16)
         return dot(ds, q_tile), dot(p.astype(jnp.bfloat16), g_tile), ds
@@ -144,21 +175,21 @@
     k_t[...] = k_ref[...].astype(jnp.float32).T.astype(jnp.bfloat16)
     own_k[...] = jnp.zeros_like(own_k)
     own_v[...] = jnp.zeros_like(own_v)
-    load_q.wait()
-    load_g.wait()
+    for copy in loads:
+        copy.wait()
     tile = LANES if rows % LANES == 0 else rows
 
     def own_head(h, carry):
         dq_t[columns(h), :] = jnp.zeros((head, rows), jnp.float32)
         for low in range(0, rows, tile):
             u = slice(low, low + tile)
+            t = pl.ds(pl.multiple_of(h * rows + low, tile), rows - low)
             dk, dv, ds = grads(
-                h,
                 k_ref[u, :],
                 v_ref[u, :],
                 bias[u, low:],
-                q[low:, columns(h)],
-                g[low:, columns(h)],
+                q[t, :],
+                g[t, :],
                 lse2[pl.ds(h, 1), :][:, low:],
                 delta_ref[pl.ds(h, 1), :][:, low:],
             )
@@ -167,35 +198,48 @@
             dq_t[columns(h), low:] += dot(k_t[:, u], ds)
         return carry
 
-    lax.fori_loop(0, heads, own_head, 0)
-
-    def cross(d, carry):
+    lax.fori_loop(0, heads, own_head, 0, unroll=2)
+
+    def cross(step, carry):
+        d = 2 * (step + 1) - lax.div(step, 2) * (4 * step - 5)
+
         @pl.when(me >= d)
         def _():
-            for copy in kv_copies(d):
+            for copy in kv_copies(own, d, partner, 0):
                 copy.wait_recv()
+
+            @pl.when(step == 0)
+            def _():
+                send((3, 4))
+
+            @pl.when(step == 1)
+            def _():
+                send((5,))
+
             set_bias(d)
             k_t[...] = kbuf[d - 1].astype(jnp.float32).T.astype(jnp.bfloat16)
             acc_k[...] = jnp.zeros_like(acc_k)
             acc_v[...] = jnp.zeros_like(acc_v)
 
-            def one_head(h, inner):
+            def one_pack(n, inner):
+                h = n * pack
                 dk, dv, ds = grads(
-                    h,
                     kbuf[d - 1],
                     vbuf[d - 1],
-                    bias[...],
-                    q[:, columns(h)],
-                    g[:, columns(h)],
-                    lse2[pl.ds(h, 1), :],
-                    delta_ref[pl.ds(h, 1), :],
+                    jnp.concatenate([bias[...]] * pack, axis=1),
+                    q[stacked(h), :],
+                    g[stacked(h), :],
+                    head_rows(lse2, h),
+                    head_rows(delta_ref, h),
                 )
                 acc_k[...] += dk
                 acc_v[...] += dv
-                dq_t[columns(h), :] += dot(k_t[...], ds)
+                dq = dot(k_t[...], ds)
+                for m in range(pack):
+                    dq_t[columns(h + m), :] += dq[:, m * rows : (m + 1) * rows]
                 return inner
 
-            lax.fori_loop(0, heads, one_head, 0)
+            lax.fori_loop(0, heads // pack, one_pack, 0, unroll=UNROLL)
             out_k[d - 1] = (acc_k[...] * scale).astype(jnp.bfloat16)
             out_v[d - 1] = acc_v[...].astype(jnp.bfloat16)
             for copy in grad_copies(d):
@@ -203,14 +247,21 @@
 
         return carry
 
-    lax.fori_loop(1, REACH + 1, cross, 0)
+    lax.fori_loop(0, REACH, cross, 0)
 
     for h in range(heads):
         c = slice(h * head, (h + 1) * head)
         dq_ref[:, c] = (dq_t[c, :] * scale).T.astype(jnp.bfloat16)
 
     own_k[...] = own_k[...] * scale
-    for d in range(1, REACH + 1):
+    for used, copies in routes:
+
+        @pl.when(used)
+        def _():
+            for copy in copies:
+                copy.wait_send()
+
+    for d in (2, 4, 3, 1):
 
         @pl.when(me + d < count)
         def _():
@@ -218,9 +269,6 @@
                 copy.wait_recv()
             own_k[...] += in_k[d - 1].astype(jnp.float32)
             own_v[...] += in_v[d - 1].astype(jnp.float32)
-            for copy in kv_copies(d):
-                copy.wait_send()
-
         @pl.when(me >= d)
         def _():
             for copy in grad_copies(d):
@@ -233,6 +281,7 @@
 def shards(count, per_seq, query_rows, key_rows, value_rows, out_grad, logsumexp, row_delta, doc_lengths):
     rows, head = key_rows.shape
     wide = query_rows.shape
+    heads = wide[1] // head
     half, full = jnp.bfloat16, jnp.float32
     vmem = pl.BlockSpec(memory_space=pltpu.VMEM)
     hbm = pl.BlockSpec(memory_space=pl.ANY)
@@ -246,8 +295,8 @@
         in_specs=[pl.BlockSpec(memory_space=pltpu.SMEM), hbm, hbm, vmem, vmem, vmem, vmem],
         out_specs=(vmem, vmem, vmem),
         scratch_shapes=[
-            pltpu.VMEM(wide, half),
-            pltpu.VMEM(wide, half),
+            pltpu.VMEM((heads * rows, head), half),
+            pltpu.VMEM((heads * rows, head), half),
             pltpu.VMEM((REACH, rows, head), half),
             pltpu.VMEM((REACH, rows, head), half),
             pltpu.VMEM((head, rows), half),
@@ -262,8 +311,8 @@
             pltpu.VMEM((REACH, rows, head), half),
             pltpu.VMEM((REACH, rows, head), half),
             pltpu.VMEM((REACH, rows, head), half),
-            pltpu.SemaphoreType.DMA((2,)),
-            pltpu.SemaphoreType.DMA((2, REACH)),
+            pltpu.SemaphoreType.DMA((2, heads)),
+            pltpu.SemaphoreType.DMA((2, 5)),
             pltpu.SemaphoreType.DMA((2, REACH)),
             pltpu.SemaphoreType.DMA((2, REACH)),
             pltpu.SemaphoreType.DMA((2, REACH)),

time: 47.2 us -> 39 us (0.83)
  Pallas kernels: 42.4 us -> 34.4 us
    pallas_call x1, Pallas kernels: 42.4 us -> 34.4 us  [shards(): pl.pallas_call(functools.partial(kernel, count, per_seq), out_shape=(jax....]
where the time goes in v2:
time: 39 us; the launch traced here: 38.7 us
  Pallas kernels  34.4 us (88%)
  local copies, waits for them, and re-layouts  3.67 us (9%)
  between operations  0.65 us (2%)
    pallas_call x1, Pallas kernels, shards(): pl.pallas_call(functools.partial(kernel, count, per_seq), out_shape=(jax....  34.4 us
    unnamed x7, local copies, waits for them, and re-layouts  3.67 us

profile of v2, /device:TPU:7, one launch (start us, length us, event | category | flops | bytes accessed | tf_op | source)
XLA Modules:
  0.0 38.7 jit_solution(276367849751945486)
XLA Ops:
  0.6 34.4 %shard_map.94 = (bf16[384,1024]{1,0:T(8,128)(2,1)}, bf16[384,128]{1,0:T(8,128)(2,1)}, bf16[384,128]{1,0:T(8,128)(2,1)}) custom-call(s32[31]{0:T(128)} %lens_ref.1, bf16[384,1024]{1,0:T(8,128)(2,1)} %q_hbm.1, bf16[384,1024]{1,0:T(8,128)(2,1)} %g_hbm.1, bf16[384,128]{1,0:T(8,128)(2,1)} %k_ref.1, bf16[384,128]{1,0:T(8,128)(2,1)} %v_ref.1, f32[8,384]{1,0:T(8,128)} %lse_ref.1, ...), custom_call_target="tpu_custom_call" | custom-call | tf_op jit(solution)/shard_map/pallas_call | solution.py:288
  35.1 0.0 copy-start.1
  35.1 2.1 %copy.13 = bf16[384,1024]{1,0:T(8,128)(2,1)} copy(bf16[384,1024]{1,0:T(8,128)(2,1)} %get-tuple-element.6) | data formatting | bytes 1572864
  37.2 0.0 copy-done.1
  37.2 0.0 copy-start
  37.2 0.6 %copy.14 = bf16[384,128]{1,0:T(8,128)(2,1)} copy(bf16[384,128]{1,0:T(8,128)(2,1)S(1)} %copy-done.1) | data formatting | bytes 196608
  37.8 0.3 copy-done
  38.1 0.6 %copy.15 = bf16[384,128]{1,0:T(8,128)(2,1)} copy(bf16[384,128]{1,0:T(8,128)(2,1)S(1)} %copy-done) | data formatting | bytes 196608
Async XLA Ops:
  35.1 2.1 %copy-start.1 = (bf16[384,128]{1,0:T(8,128)(2,1)S(1)}, bf16[384,128]{1,0:T(8,128)(2,1)}, u32[]{:S(2)}) copy-start(bf16[384,128]{1,0:T(8,128)(2,1)} %get-tuple-element.7) | copy-start | bytes 294916
  37.2 0.9 %copy-start = (bf16[384,128]{1,0:T(8,128)(2,1)S(1)}, bf16[384,128]{1,0:T(8,128)(2,1)}, u32[]{:S(2)}) copy-start(bf16[384,128]{1,0:T(8,128)(2,1)} %get-tuple-element.8) | copy-start | bytes 294916

commit v3 on v2

--- a/solution.py
+++ b/solution.py
@@ -10,7 +10,7 @@
 
 REACH = 4
 LANES = 128
-UNROLL = 2
+UNROLL = 4
 LOG2E = math.log2(math.e)
 MESH = pl.DeviceIdType.MESH
 
@@ -278,6 +278,12 @@
     dv_ref[...] = own_v[...].astype(jnp.bfloat16)
 
 
+def pass_on(dq_ref, dk_ref, dv_ref, dq_out, dk_out, dv_out):
+    dq_out[...] = dq_ref[...]
+    dk_out[...] = dk_ref[...]
+    dv_out[...] = dv_ref[...]
+
+
 def shards(count, per_seq, query_rows, key_rows, value_rows, out_grad, logsumexp, row_delta, doc_lengths):
     rows, head = key_rows.shape
     wide = query_rows.shape
@@ -285,7 +291,7 @@
     half, full = jnp.bfloat16, jnp.float32
     vmem = pl.BlockSpec(memory_space=pltpu.VMEM)
     hbm = pl.BlockSpec(memory_space=pl.ANY)
-    return pl.pallas_call(
+    grads = pl.pallas_call(
         functools.partial(kernel, count, per_seq),
         out_shape=(
             jax.ShapeDtypeStruct(wide, half),
@@ -319,6 +325,12 @@
         ],
         compiler_params=pltpu.CompilerParams(collective_id=0, has_side_effects=True),
     )(doc_lengths, query_rows, out_grad, key_rows, value_rows, logsumexp, row_delta)
+    return pl.pallas_call(
+        pass_on,
+        out_shape=tuple(jax.ShapeDtypeStruct(part.shape, part.dtype) for part in grads),
+        in_specs=[vmem] * 3,
+        out_specs=(vmem,) * 3,
+    )(*grads)
 
 
 def solution(mesh):

time: 39 us -> 37.1 us (0.951)
  local copies, waits for them, and re-layouts: 3.67 us -> 0 us
  Pallas kernels: 34.4 us -> 36.3 us
    unnamed x7 -> x0, local copies, waits for them, and re-layouts: 3.67 us -> none
    pallas_call x0 -> x1, Pallas kernels: none -> 2.15 us  [shards(): pl.pallas_call(pass_on, out_shape=tuple((jax.ShapeDtypeStruct(part.shape,...]
where the time goes in v3:
time: 37.1 us; the launch traced here: 36.9 us
  Pallas kernels  36.3 us (98%)
  between operations  0.64 us (2%)
    pallas_call x1, Pallas kernels, shards(): pl.pallas_call(functools.partial(kernel, count, per_seq), out_shape=(jax....  34.1 us
    pallas_call x1, Pallas kernels, shards(): pl.pallas_call(pass_on, out_shape=tuple((jax.ShapeDtypeStruct(part.shape,...  2.15 us

profile of v3, /device:TPU:7, one launch (start us, length us, event | category | flops | bytes accessed | tf_op | source)
XLA Modules:
  0.0 36.9 jit_solution(6741091907764791452)
XLA Ops:
  0.6 34.1 %shard_map.94 = (bf16[384,1024]{1,0:T(8,128)(2,1)}, bf16[384,128]{1,0:T(8,128)(2,1)}, bf16[384,128]{1,0:T(8,128)(2,1)}) custom-call(s32[31]{0:T(128)} %lens_ref.1, bf16[384,1024]{1,0:T(8,128)(2,1)} %q_hbm.1, bf16[384,1024]{1,0:T(8,128)(2,1)} %g_hbm.1, bf16[384,128]{1,0:T(8,128)(2,1)} %k_ref.1, bf16[384,128]{1,0:T(8,128)(2,1)} %v_ref.1, f32[8,384]{1,0:T(8,128)} %lse_ref.1, ...), custom_call_target="tpu_custom_call" | custom-call | tf_op jit(solution)/shard_map/pallas_call | solution.py:294
  34.7 2.2 %shard_map.95 = (bf16[384,1024]{1,0:T(8,128)(2,1)}, bf16[384,128]{1,0:T(8,128)(2,1)}, bf16[384,128]{1,0:T(8,128)(2,1)}) custom-call(bf16[384,1024]{1,0:T(8,128)(2,1)} %get-tuple-element.6.dq_ref, bf16[384,128]{1,0:T(8,128)(2,1)} %get-tuple-element.7.dk_ref, bf16[384,128]{1,0:T(8,128)(2,1)} %get-tuple-element.8.dv_ref), custom_call_target="tpu_custom_call" | custom-call | tf_op jit(solution)/shard_map/pallas_call | solution.py:328
